TPU v7x, 8 devices: a whole 2x2x1 slice. The times are simulated.
8 devices in a mesh: dp: 1 (over z), tp: 2 (over y), cp: 4 (over x, core).
Axes of the slice: x: 2, y: 2, z: 1, core: 2. Of those that a mesh axis runs over, the one named last changes fastest.
Arguments:
- x_tokens: bfloat16 [512, 5120], P(('dp', 'cp', 'tp'))
- w_q: bfloat16 [5120, 40, 128], P(None, 'tp')
- w_k: bfloat16 [5120, 40, 128], P(None, 'tp')
- w_v: bfloat16 [5120, 40, 128], P(None, 'tp')
- w_o: bfloat16 [40, 128, 5120], P('tp')
Outputs:
- output: bfloat16 [512, 5120], P(('dp', 'cp', 'tp'))
All inputs are finite; a program needn't handle non-finite values.
Results may differ from a plain program's by a relative error of at most 0.00536832.
Values are sent between devices in bfloat16 or wider.
A program may use at most 1 GiB of HBM per device.

v0:
```python
import functools

import jax
import jax.numpy as jnp
from jax import lax
from jax.experimental import pallas as pl
from jax.experimental.pallas import tpu as pltpu
from jax.sharding import PartitionSpec as P

BF16, F32 = jnp.bfloat16, jnp.float32
NEG_BIG = -1e30
D = 5120
E = 128
HEADS = 5
HE = HEADS * E
NQKV = 3 * HE
BLK = 64
HALF = BLK // 2
NK = 10
KC = D // NK
LATE = NK // 2
DIAG_X = 7
NOUT = 10
NC = D // NOUT
MESH = pl.DeviceIdType.MESH


def remote(src, dst, send_sem, recv_sem, dev):
    return pltpu.make_async_remote_copy(src_ref=src, dst_ref=dst, send_sem=send_sem, recv_sem=recv_sem, device_id=dev, device_id_type=MESH)


def drain(ref, sem):
    pltpu.make_async_copy(ref, ref, sem).wait()


def kernel(x_hbm, wq_hbm, wk_hbm, wv_hbm, wo_hbm, y_ref, xs, w, wo, qkv, acc, osend, ofull, ysend, yrecv,
           in_sem, x_send, sib_recv, direct_recv, fwd_recv, dg_send, o_send_sem, o_recv_sem,
           y_send_sem, y_recv_sem):
    cp, tp = lax.axis_index('cp'), lax.axis_index('tp')
    x, c = cp // 2, cp % 2
    sib = {'cp': 2 * x + 1 - c, 'tp': tp}
    xn = {'cp': 2 * (1 - x) + c, 'tp': tp}
    xo = {'cp': 2 * (1 - x) + 1 - c, 'tp': tp}
    yn = {'cp': cp, 'tp': 1 - tp}

    def rows(group, core):
        return pl.ds(pl.multiple_of(group * 128 + core * BLK, BLK), BLK)

    def x_in(k):
        return pltpu.make_async_copy(x_hbm.at[:, pl.ds(k * KC, KC)], xs.at[k, rows(0, c), :], in_sem)

    def w_in(j):
        src = (wq_hbm, wk_hbm, wv_hbm)[j // HEADS].at[cp * HEADS + j % HEADS]
        return pltpu.make_async_copy(src, w.at[:, pl.ds(j * E, E)], in_sem)

    def wo_in(n):
        return pltpu.make_async_copy(wo_hbm.at[:, pl.ds(n * NC, NC)], wo.at[n], in_sem)

    for k in range(NK):
        x_in(k).start()
    barrier = pltpu.get_barrier_semaphore()
    for dev in (sib, xn, xo, yn):
        pl.semaphore_signal(barrier, inc=1, device_id=dev, device_id_type=MESH)
    drain(xs.at[:, rows(0, c), :], in_sem)
    for j in range(3 * HEADS):
        w_in(j).start()
    with jax.named_scope('barrier'):
        pl.semaphore_wait(barrier, 4)

    def group_of(kind, t):
        return (1, 2 + t, 3 - t, 0)[kind]

    def own(k, kind):
        dev, t = ((yn, 1 - tp), (xn, tp), None, (sib, tp))[kind]
        return remote(xs.at[k, rows(0, c), :], xs.at[k, rows(group_of(kind, t), c), :], x_send, sib_recv if kind == 3 else direct_recv.at[kind, k], dev)

    def diag(k, over_y):
        dev, src, t = (yn, group_of(1, tp), 1 - tp) if over_y else (xn, group_of(0, tp), tp)
        return remote(xs.at[k, rows(src, c), :], xs.at[k, rows(group_of(2, t), c), :], dg_send, direct_recv.at[2, k], dev)

    def half_diag(over_y):
        dev, src, t = (yn, group_of(1, tp), 1 - tp) if over_y else (xn, group_of(0, tp), tp)
        k, first = LATE - 1, 0 if over_y else HALF
        return remote(xs.at[k, pl.ds(pl.multiple_of(src * 128 + c * BLK + first, HALF), HALF), :],
                      xs.at[k, pl.ds(pl.multiple_of(group_of(2, t) * 128 + c * BLK + first, HALF), HALF), :],
                      dg_send, direct_recv.at[2, k], dev)

    def fwd(k, kind):
        sl = rows(group_of(kind, tp), c)
        second = NK + k % LATE
        sem = (k, jnp.where(tp == 0, k, second), jnp.where(tp == 0, second, NK + LATE + k))[kind]
        return remote(xs.at[k, sl, :], xs.at[k, sl, :], x_send, fwd_recv.at[sem], sib)

    def direct_wait(k, kind):
        drain(xs.at[k, rows(group_of(kind, tp), c), :], direct_recv.at[kind, k])

    def sends_diag_x(k):
        return jnp.where(tp == 0, k >= LATE, k < DIAG_X)

    def sends_half_x(k):
        return (tp == 0) & (x == 0) & (k == LATE - 1)

    def sends_diag_y(k):
        return jnp.where(tp == 0, k >= DIAG_X, k < LATE - x)

    def sends_half_y(k):
        return (tp == 1) & (x == 1) & (k == LATE - 1)

    def handle(k, kind):
        direct_wait(k, kind)
        fwd(k, kind).start()
        if kind == 0:
            @pl.when(sends_diag_x(k))
            def _():
                diag(k, False).start()

            @pl.when(sends_half_x(k))
            def _():
                half_diag(False).start()
        if kind == 1:
            @pl.when(sends_diag_y(k))
            def _():
                diag(k, True).start()

            @pl.when(sends_half_y(k))
            def _():
                half_diag(True).start()

    for k in range(NK):
        if k < LATE:
            own(k, 1).start()
        else:
            @pl.when(tp == 0)
            def _():
                own(k, 1).start()
        own(k, 0).start()
        own(k, 3).start()

    acc[...] = jnp.zeros_like(acc)

    def nat(xx, core, t):
        b = 2 * xx + core
        return jnp.where(t == 0, b, 7 - b) * BLK

    nat_of = [nat(x, 0, tp), nat(x, 1, tp), nat(x, 0, 1 - tp), nat(x, 1, 1 - tp),
              nat(1 - x, 0, 0), nat(1 - x, 1, 0), nat(1 - x, 0, 1), nat(1 - x, 1, 1)]

    def put_qkv(slot, col, n, val):
        qkv[pl.ds(pl.multiple_of(nat_of[slot], BLK), BLK), pl.ds(col, n)] = val.astype(BF16)

    NSTEPS = ((0, 512), (512, 512), (1024, 512), (1536, 384))

    def own_chip():
        with jax.named_scope('wait_sib'):
            drain(xs.at[:, rows(0, c), :], sib_recv)
        with jax.named_scope('wait_w'):
            drain(w, in_sem)
        for n in range(NOUT):
            wo_in(n).start()
        for col, n in NSTEPS:
            val = jnp.dot(xs[0, 0:128, :], w[0:KC, col:col + n], preferred_element_type=F32)
            for k in range(1, NK):
                val += jnp.dot(xs[k, 0:128, :], w[k * KC:(k + 1) * KC, col:col + n], preferred_element_type=F32)
            put_qkv(0, col, n, val[:BLK])
            put_qkv(1, col, n, val[BLK:])

    def accumulate(chunks, row, m, arow):
        for col, n in NSTEPS:
            val = acc[arow:arow + m, col:col + n]
            for k in chunks:
                val += jnp.dot(xs[k, row:row + m, :], w[pl.ds(pl.multiple_of(k * KC, KC), KC), col:col + n], preferred_element_type=F32)
            acc[arow:arow + m, col:col + n] = val

    def diag_order(m):
        return jnp.where(m < 5, m, jnp.where(m % 2 == 1, 7 + (m - 5) // 2, 5 + (m - 6) // 2))

    def wait_fwd2(j):
        with jax.named_scope('w_fwd2'):
            drain(xs.at[0, pl.ds(384, 128), :], fwd_recv.at[NK + j])

    def pair(j):
        wait_fwd2(j)
        with jax.named_scope('acc_b'):
            accumulate((j, j + LATE), 384, 128, 256)

    @pl.loop(0, NK + LATE)
    def _(i):
        @pl.when(i < NK)
        def _():
            with jax.named_scope('h_y'):
                handle(i, 0)

        @pl.when(i < jnp.where(tp == 0, NK, LATE))
        def _():
            with jax.named_scope('h_x'):
                handle(i, 1)

        @pl.when((tp == 0) & (i >= NK) & (i < NK + LATE))
        def _():
            with jax.named_scope('h_d2'):
                handle(i - NK, 2)
                handle(i - NK + LATE, 2)

        @pl.when((tp == 1) & (i >= 5) & (i < NK + 3))
        def _():
            with jax.named_scope('h_d'):
                handle(diag_order(jnp.where(i == NK + 2, 8, i - 5)), 2)

                @pl.when(i > NK)
                def _():
                    handle(diag_order(jnp.where(i == NK + 2, 9, 7)), 2)

        @pl.when(i == 2)
        def _():
            own_chip()

        @pl.when((i >= 2) & (i < NK + 2))
        def _():
            k = i - 2

            @pl.when(tp == 0)
            def _():
                with jax.named_scope('w_fwd'):
                    drain(xs.at[k, pl.ds(128, 128), :], fwd_recv.at[k])
                with jax.named_scope('acc_a'):
                    accumulate((k,), 128, 256, 0)

            @pl.when(tp == 1)
            def _():
                with jax.named_scope('w_fwd'):
                    drain(xs.at[k, pl.ds(128, BLK), :], fwd_recv.at[k])
                with jax.named_scope('acc_y'):
                    accumulate((k,), 128, 128, 0)

        def wait_d(k):
            with jax.named_scope('w_fwd'):
                drain(xs.at[k, pl.ds(256, BLK), :], fwd_recv.at[NK + LATE + k])

        @pl.when((tp == 1) & (i >= 6) & (i < NK + 2))
        def _():
            k = diag_order(i - 6)
            wait_d(k)
            with jax.named_scope('acc_d'):
                accumulate((k,), 256, 128, 128)

        @pl.when((tp == 1) & (i >= NK + 2) & (i < NK + 4))
        def _():
            k, k2 = i - NK + 3, i - NK + 6
            wait_d(k)
            wait_d(k2)
            with jax.named_scope('acc_d'):
                accumulate((k, k2), 256, 128, 128)

        @pl.when((tp == 0) & (i > NK) & (i < NK + LATE))
        def _():
            pair(i - NK - 1)

    for col, n in NSTEPS:
        for s in range(4):
            put_qkv(2 + s, col, n, acc[s * BLK:(s + 1) * BLK, col:col + n])

    def rest_of_rows():
        @pl.when(tp == 1)
        def _():
            @pl.loop(0, LATE)
            def _(j):
                with jax.named_scope('h_x2'):
                    handle(j + LATE, 1)

                @pl.when(j > 0)
                def _():
                    pair(j - 1)

        wait_fwd2(LATE - 1)
        with jax.named_scope('acc_b'):
            for col, n in NSTEPS:
                val = acc[256:384, col:col + n]
                for k in (LATE - 1, NK - 1):
                    val += jnp.dot(xs[k, 384:512, :], w[k * KC:(k + 1) * KC, col:col + n], preferred_element_type=F32)
                for s in range(2):
                    put_qkv(6 + s, col, n, val[s * BLK:(s + 1) * BLK])

    inv_sqrt = E ** -0.5

    def o_copy(b, half, dev_cp):
        lohi, part = b // 4, pl.ds(half * HALF, HALF)
        return remote(osend.at[b, part], ofull.at[lohi, part, pl.ds(pl.multiple_of(cp * HE, E), HE)],
                      o_send_sem, o_recv_sem.at[jnp.where(lohi == tp, 4, 2 * half + jnp.where(x == dev_cp // 2, 0, 1))], {'cp': dev_cp, 'tp': tp})

    def attend(b):
        length = 128 * (b // 2 + 1)
        ri = lax.broadcasted_iota(jnp.int32, (BLK, 128), 0) + BLK * (b % 2)
        ci = lax.broadcasted_iota(jnp.int32, (BLK, 128), 1)
        mask = ci <= ri
        heads = range(HEADS)
        q = [qkv[b * BLK:(b + 1) * BLK, h * E:(h + 1) * E] for h in heads]
        kk = [qkv[0:length, HE + h * E:HE + (h + 1) * E] for h in heads]
        v = [qkv[0:length, 2 * HE + h * E:2 * HE + (h + 1) * E] for h in heads]
        s = [lax.dot_general(q[h], kk[h], (((1,), (1,)), ((), ())), preferred_element_type=F32) * inv_sqrt for h in heads]
        last = [jnp.where(mask, s[h][:, length - 128:], NEG_BIG) for h in heads]
        s = [last[h] if length == 128 else jnp.concatenate([s[h][:, :length - 128], last[h]], axis=1) for h in heads]
        m = [jnp.max(s[h], axis=-1, keepdims=True) for h in heads]
        p = [jnp.exp(s[h] - m[h]) for h in heads]
        l = [jnp.sum(p[h], axis=-1, keepdims=True) for h in heads]
        o = [jnp.dot(p[h].astype(BF16), v[h], preferred_element_type=F32) for h in heads]
        for h in heads:
            osend[b, :, h * E:(h + 1) * E] = (o[h] / l[h]).astype(BF16)
    def send_o(b, half):
        r = jnp.where(b < 4, b, 7 - b)

        @pl.when(cp == r)
        def _():
            part = pl.ds(half * HALF, HALF)
            ofull[b // 4, part, pl.ds(pl.multiple_of(cp * HE, E), HE)] = osend[b, part]

        @pl.when(cp != r)
        def _():
            o_copy(b, half, r).start()

    def wait_o(half, far):
        drain(osend.at[pl.ds(0, 1 + far), pl.ds(0, HALF)], o_recv_sem.at[2 * half + far])

    def attend_blocks(hi):
        def block_at(step):
            first, odd = step < 2, step % 2
            pair = jnp.where(hi, jnp.where(first, 2 + x, 3 - x), jnp.where(first, 1 - x, x))
            return 2 * pair + jnp.where(hi, odd, 1 - odd)

        @pl.loop(0, 4)
        def _(step):
            block = block_at(step)
            for b in range(8):
                @pl.when(block == b)
                def _():
                    with jax.named_scope(f'attend{b}'):
                        attend(b)

            for at, sends in enumerate((((0, 0),), ((0, 1),), ((1, 0), (1, 1), (2, 0), (2, 1)), ((3, 0), (3, 1)))):
                @pl.when(step == at)
                def _():
                    for which, half in sends:
                        send_o(block_at(which), half)

    away, home = 1 - tp, tp

    def y_copy(n, half):
        part = pl.ds(half * HALF, HALF)
        return remote(ysend.at[n, part], yrecv.at[n, part], y_send_sem, y_recv_sem.at[n], yn)

    top, bottom = slice(0, HALF), slice(HALF, BLK)

    def project_away():
        near = pl.ds(pl.multiple_of(2 * x * HE, E), 2 * HE)
        far = pl.ds(pl.multiple_of(2 * (1 - x) * HE, E), 2 * HE)
        drain(wo, in_sem)
        with jax.named_scope('wait_o_away'):
            wait_o(0, 0)
        with jax.named_scope('proj'):
            ysend[0, top] = jnp.dot(ofull[away, top, near], wo[0, near, :], preferred_element_type=F32)
        with jax.named_scope('wait_o_away'):
            wait_o(0, 1)
        with jax.named_scope('proj'):
            ysend[0, top] += jnp.dot(ofull[away, top, far], wo[0, far, :], preferred_element_type=F32)
        y_copy(0, 0).start()

        @pl.loop(1, NOUT)
        def _(n):
            with jax.named_scope('proj'):
                ysend[n, top] = jnp.dot(ofull[away, top], wo[n], preferred_element_type=F32)
            y_copy(n, 0).start()

    def project_rest():
        with jax.named_scope('wait_o_away'):
            wait_o(1, 0)
            wait_o(1, 1)

        @pl.loop(0, NOUT)
        def _(n):
            with jax.named_scope('proj'):
                ysend[n, bottom] = jnp.dot(ofull[away, bottom], wo[n], preferred_element_type=F32)
            y_copy(n, 1).start()

    @pl.loop(0, 4)
    def _(stage):
        @pl.when(stage == 2 * tp)
        def _():
            rest_of_rows()

        @pl.when((stage == 1 - tp) | (stage == 3))
        def _():
            attend_blocks((stage < 2) == (tp == 0))

            @pl.when((tp == 1) & (stage == 0))
            def _():
                for k in range(LATE, NK):
                    own(k, 1).start()

        @pl.when(stage == 2 - tp)
        def _():
            project_away()

            @pl.when((tp == 1) | (c == 0))
            def _():
                project_rest()

    with jax.named_scope('wait_o_home'):
        drain(osend.at[pl.ds(0, 3)], o_recv_sem.at[4])

    @pl.when((tp == 0) & (c == 1))
    def _():
        project_rest()

    def kept(n):
        return acc.at[pl.ds(pl.multiple_of(n % 6 * BLK, BLK), BLK), pl.ds(pl.multiple_of(n // 6 * NC, NC), NC)]

    @pl.loop(0, NOUT)
    def _(n):
        kept(n)[...] = jnp.dot(ofull[home], wo[n], preferred_element_type=F32)

    @pl.loop(0, NOUT)
    def _(n):
        with jax.named_scope('wait_y'):
            drain(yrecv.at[n], y_recv_sem.at[n])
        y_ref[:, pl.ds(pl.multiple_of(n * NC, NC), NC)] = (kept(n)[...] + yrecv[n]).astype(BF16)

    drain(xs.at[:, pl.ds(0, 6 * BLK), :], x_send)
    for t in range(2):
        for xx in range(2):
            over_x = DIAG_X * BLK if t else (NK - LATE) * BLK + (1 - xx) * HALF
            over_y = LATE * BLK - xx * HALF if t else (NK - DIAG_X) * BLK

            @pl.when((tp == t) & (x == xx))
            def _():
                drain(xs.at[pl.ds(0, 2), pl.ds(0, (over_x + over_y) // 2), :], dg_send)
    drain(osend.at[pl.ds(0, 6)], o_send_sem)
    drain(ysend, y_send_sem)


def solution(mesh):
    def device_fn(x_loc, w_q, w_k, w_v, w_o):
        dma = pltpu.SemaphoreType.DMA
        heads_major = [jnp.transpose(t, (1, 0, 2)) for t in (w_q, w_k, w_v)]
        return pl.pallas_call(
            kernel,
            name='attention_layer',
            out_shape=pltpu.VMEM((BLK, D), BF16),
            in_specs=[pl.BlockSpec(memory_space=pl.ANY)] * 5,
            out_specs=pl.BlockSpec(memory_space=pltpu.VMEM),
            scratch_shapes=[
                pltpu.VMEM((NK, 512, KC), BF16),
                pltpu.VMEM((D, NQKV), BF16),
                pltpu.VMEM((NOUT, 20 * E, NC), BF16),
                pltpu.VMEM((512, NQKV), BF16),
                pltpu.VMEM((384, NQKV), F32),
                pltpu.VMEM((8, BLK, HE), BF16),
                pltpu.VMEM((2, BLK, 20 * E), BF16),
                pltpu.VMEM((NOUT, BLK, NC), F32),
                pltpu.VMEM((NOUT, BLK, NC), F32),
                dma, dma, dma, dma((3, NK)), dma((2 * NK + LATE,)), dma,
                dma, dma((5,)),
                dma, dma((NOUT,)),
            ],
            compiler_params=pltpu.CompilerParams(collective_id=0, has_side_effects=True, vmem_limit_bytes=64 * 1000 * 1000),
        )(x_loc, *heads_major, w_o.reshape(20 * E, D))

    seq_spec = P(('dp', 'cp', 'tp'), None)
    head_spec = P(None, 'tp', None)
    return jax.shard_map(device_fn, mesh=mesh, in_specs=(seq_spec, head_spec, head_spec, head_spec, P('tp', None, None)), out_specs=seq_spec, check_vma=False)
```

profile of v0, /device:TPU:1, one launch (start us, length us, event | category | flops | bytes accessed | tf_op | source)
XLA Modules:
  0.0 62.2 jit_solution(11139522824051785981)
XLA Ops:
  0.0 61.3 %attention_layer.1 = bf16[64,5120]{1,0:T(8,128)(2,1)S(1)} custom-call(bf16[64,5120]{1,0:T(8,128)(2,1)} %x_hbm.1, bf16[20,5120,128]{2,1,0:T(8,128)(2,1)} %bitcast.4, bf16[20,5120,128]{2,1,0:T(8,128)(2,1)} %bitcast.5, bf16[20,5120,128]{2,1,0:T(8,128)(2,1)} %bitcast.6, bf16[2560,5120]{1,0:T(8,128)(2,1)} %bitcast.7), custom_call_target="tpu_custom_call" | custom-call | tf_op jit(solution)/shard_map/attention_layer/pallas_call | solution.py:443
  61.3 0.8 %copy.7 = bf16[64,5120]{1,0:T(8,128)(2,1)} copy(bf16[64,5120]{1,0:T(8,128)(2,1)S(1)} %attention_layer.1) | data formatting | bytes 1310720
where the time goes:
time: 62.3 us; the launch traced here: 62.2 us
  Pallas kernels  61.3 us (98%)
  local copies, waits for them, and re-layouts  0.84 us (1%)
    pallas_call x1, Pallas kernels, device_fn(): pl.pallas_call(kernel, name='attention_layer', out_shape=pltpu.VMEM((BLK,...  61.3 us

commit v1 on v0

--- a/solution.py
+++ b/solution.py
@@ -34,7 +34,7 @@
 
 
 def kernel(x_hbm, wq_hbm, wk_hbm, wv_hbm, wo_hbm, y_ref, xs, w, wo, qkv, acc, osend, ofull, ysend, yrecv,
-           in_sem, x_send, sib_recv, direct_recv, fwd_recv, dg_send, o_send_sem, o_recv_sem,
+           in_sem, in_sem2, x_send, sib_recv, direct_recv, fwd_recv, dg_send, o_send_sem, o_recv_sem,
            y_send_sem, y_recv_sem):
     cp, tp = lax.axis_index('cp'), lax.axis_index('tp')
     x, c = cp // 2, cp % 2
@@ -47,7 +47,7 @@
         return pl.ds(pl.multiple_of(group * 128 + core * BLK, BLK), BLK)
 
     def x_in(k):
-        return pltpu.make_async_copy(x_hbm.at[:, pl.ds(k * KC, KC)], xs.at[k, rows(0, c), :], in_sem)
+        return pltpu.make_async_copy(x_hbm.at[:, pl.ds(k * KC, KC)], xs.at[k, rows(0, c), :], in_sem if k < 2 else in_sem2)
 
     def w_in(j):
         src = (wq_hbm, wk_hbm, wv_hbm)[j // HEADS].at[cp * HEADS + j % HEADS]
@@ -61,9 +61,7 @@
     barrier = pltpu.get_barrier_semaphore()
     for dev in (sib, xn, xo, yn):
         pl.semaphore_signal(barrier, inc=1, device_id=dev, device_id_type=MESH)
-    drain(xs.at[:, rows(0, c), :], in_sem)
-    for j in range(3 * HEADS):
-        w_in(j).start()
+    drain(xs.at[pl.ds(0, 2), rows(0, c), :], in_sem)
     with jax.named_scope('barrier'):
         pl.semaphore_wait(barrier, 4)
 
@@ -127,6 +125,10 @@
                 half_diag(True).start()
 
     for k in range(NK):
+        if k == 2:
+            drain(xs.at[pl.ds(2, NK - 2), rows(0, c), :], in_sem2)
+            for j in range(3 * HEADS):
+                w_in(j).start()
         if k < LATE:
             own(k, 1).start()
         else:
@@ -456,7 +458,7 @@
                 pltpu.VMEM((2, BLK, 20 * E), BF16),
                 pltpu.VMEM((NOUT, BLK, NC), F32),
                 pltpu.VMEM((NOUT, BLK, NC), F32),
-                dma, dma, dma, dma((3, NK)), dma((2 * NK + LATE,)), dma,
+                dma, dma, dma, dma, dma((3, NK)), dma((2 * NK + LATE,)), dma,
                 dma, dma((5,)),
                 dma, dma((NOUT,)),
             ],

time: 62.3 us -> 62.3 us (level)
  no operation moved by 1% of the time
where the time goes in v1:
time: 62.3 us; the launch traced here: 62.2 us
  Pallas kernels  61.3 us (98%)
  local copies, waits for them, and re-layouts  0.84 us (1%)
    pallas_call x1, Pallas kernels, device_fn(): pl.pallas_call(kernel, name='attention_layer', out_shape=pltpu.VMEM((BLK,...  61.3 us

profile of v1, /device:TPU:1, one launch (start us, length us, event | category | flops | bytes accessed | tf_op | source)
XLA Modules:
  0.0 62.2 jit_solution(5966279326039915652)
XLA Ops:
  0.0 61.3 %attention_layer.1 = bf16[64,5120]{1,0:T(8,128)(2,1)S(1)} custom-call(bf16[64,5120]{1,0:T(8,128)(2,1)} %x_hbm.1, bf16[20,5120,128]{2,1,0:T(8,128)(2,1)} %bitcast.4, bf16[20,5120,128]{2,1,0:T(8,128)(2,1)} %bitcast.5, bf16[20,5120,128]{2,1,0:T(8,128)(2,1)} %bitcast.6, bf16[2560,5120]{1,0:T(8,128)(2,1)} %bitcast.7), custom_call_target="tpu_custom_call" | custom-call | tf_op jit(solution)/shard_map/attention_layer/pallas_call | solution.py:445
  61.3 0.8 %copy.7 = bf16[64,5120]{1,0:T(8,128)(2,1)} copy(bf16[64,5120]{1,0:T(8,128)(2,1)S(1)} %attention_layer.1) | data formatting | bytes 1310720

commit v2 on v1

--- a/solution.py
+++ b/solution.py
@@ -401,23 +401,27 @@
         def _():
             project_away()
 
-            @pl.when((tp == 1) | (c == 0))
+            @pl.when(tp == 1)
             def _():
                 project_rest()
+
+    @pl.when((tp == 0) & (c == 0))
+    def _():
+        project_rest()
 
     with jax.named_scope('wait_o_home'):
         drain(osend.at[pl.ds(0, 3)], o_recv_sem.at[4])
+
+    def kept(n):
+        return acc.at[pl.ds(pl.multiple_of(n % 6 * BLK, BLK), BLK), pl.ds(pl.multiple_of(n // 6 * NC, NC), NC)]
+
+    @pl.loop(0, NOUT)
+    def _(n):
+        kept(n)[...] = jnp.dot(ofull[home], wo[n], preferred_element_type=F32)
 
     @pl.when((tp == 0) & (c == 1))
     def _():
         project_rest()
-
-    def kept(n):
-        return acc.at[pl.ds(pl.multiple_of(n % 6 * BLK, BLK), BLK), pl.ds(pl.multiple_of(n // 6 * NC, NC), NC)]
-
-    @pl.loop(0, NOUT)
-    def _(n):
-        kept(n)[...] = jnp.dot(ofull[home], wo[n], preferred_element_type=F32)
 
     @pl.loop(0, NOUT)
     def _(n):

time: 62.3 us -> 62.3 us (level)
  no operation moved by 1% of the time
where the time goes in v2:
time: 62.3 us; the launch traced here: 62.2 us
  Pallas kernels  61.3 us (98%)
  local copies, waits for them, and re-layouts  0.84 us (1%)
    pallas_call x1, Pallas kernels, device_fn(): pl.pallas_call(kernel, name='attention_layer', out_shape=pltpu.VMEM((BLK,...  61.3 us

profile of v2, /device:TPU:1, one launch (start us, length us, event | category | flops | bytes accessed | tf_op | source)
XLA Modules:
  0.0 62.2 jit_solution(5421244665342171165)
XLA Ops:
  0.0 61.3 %attention_layer.1 = bf16[64,5120]{1,0:T(8,128)(2,1)S(1)} custom-call(bf16[64,5120]{1,0:T(8,128)(2,1)} %x_hbm.1, bf16[20,5120,128]{2,1,0:T(8,128)(2,1)} %bitcast.4, bf16[20,5120,128]{2,1,0:T(8,128)(2,1)} %bitcast.5, bf16[20,5120,128]{2,1,0:T(8,128)(2,1)} %bitcast.6, bf16[2560,5120]{1,0:T(8,128)(2,1)} %bitcast.7), custom_call_target="tpu_custom_call" | custom-call | tf_op jit(solution)/shard_map/attention_layer/pallas_call | solution.py:449
  61.3 0.8 %copy.7 = bf16[64,5120]{1,0:T(8,128)(2,1)} copy(bf16[64,5120]{1,0:T(8,128)(2,1)S(1)} %attention_layer.1) | data formatting | bytes 1310720

commit v3 on v1

--- a/solution.py
+++ b/solution.py
@@ -361,9 +361,10 @@
             ysend[0, top] = jnp.dot(ofull[away, top, near], wo[0, near, :], preferred_element_type=F32)
         with jax.named_scope('wait_o_away'):
             wait_o(0, 1)
-        with jax.named_scope('proj'):
-            ysend[0, top] += jnp.dot(ofull[away, top, far], wo[0, far, :], preferred_element_type=F32)
-        y_copy(0, 0).start()
+        for first in (0, NC // 2):
+            cols = pl.ds(first, NC // 2)
+            ysend[0, top, cols] += jnp.dot(ofull[away, top, far], wo[0, far, cols], preferred_element_type=F32)
+            remote(ysend.at[0, pl.ds(0, HALF), cols], yrecv.at[0, pl.ds(0, HALF), cols], y_send_sem, y_recv_sem.at[0], yn).start()
 
         @pl.loop(1, NOUT)
         def _(n):

time: 62.3 us -> 62.4 us (level)
  no operation moved by 1% of the time
where the time goes in v3:
time: 62.4 us; the launch traced here: 62.3 us
  Pallas kernels  61.4 us (98%)
  local copies, waits for them, and re-layouts  0.84 us (1%)
    pallas_call x1, Pallas kernels, device_fn(): pl.pallas_call(kernel, name='attention_layer', out_shape=pltpu.VMEM((BLK,...  61.4 us

profile of v3, /device:TPU:1, one launch (start us, length us, event | category | flops | bytes accessed | tf_op | source)
XLA Modules:
  0.0 62.3 jit_solution(14111871113444541288)
XLA Ops:
  0.0 61.4 %attention_layer.1 = bf16[64,5120]{1,0:T(8,128)(2,1)S(1)} custom-call(bf16[64,5120]{1,0:T(8,128)(2,1)} %x_hbm.1, bf16[20,5120,128]{2,1,0:T(8,128)(2,1)} %bitcast.4, bf16[20,5120,128]{2,1,0:T(8,128)(2,1)} %bitcast.5, bf16[20,5120,128]{2,1,0:T(8,128)(2,1)} %bitcast.6, bf16[2560,5120]{1,0:T(8,128)(2,1)} %bitcast.7), custom_call_target="tpu_custom_call" | custom-call | tf_op jit(solution)/shard_map/attention_layer/pallas_call | solution.py:446
  61.4 0.8 %copy.7 = bf16[64,5120]{1,0:T(8,128)(2,1)} copy(bf16[64,5120]{1,0:T(8,128)(2,1)S(1)} %attention_layer.1) | data formatting | bytes 1310720
